TPU v7x, 8 devices: a whole 2x2x1 slice. The times are simulated.
8 devices in a mesh: dp: 1 (over z), tp: 2 (over y), sp: 4 (over x, core).
Axes of the slice: x: 2, y: 2, z: 1, core: 2. Of those that a mesh axis runs over, the one named last changes fastest.
Arguments:
- hidden: bfloat16 [16, 1024], P('dp')
- k_cache: bfloat16 [16, 16384, 16, 64], P('dp', 'sp', 'tp')
- v_cache: bfloat16 [16, 16384, 16, 64], P('dp', 'sp', 'tp')
- lengths: int32 [16], P('dp')
- rel_table: bfloat16 [16384, 16, 64], P('sp', 'tp')
- u_bias: bfloat16 [16, 64], P('tp')
- w_bias: bfloat16 [16, 64], P('tp')
- g_attn: bfloat16 [1024], replicated
- w_query: bfloat16 [1024, 16, 64], P(None, 'tp')
- w_key: bfloat16 [1024, 16, 64], P(None, 'tp')
- w_value: bfloat16 [1024, 16, 64], P(None, 'tp')
- w_out: bfloat16 [16, 64, 1024], P('tp')
- g_mlp: bfloat16 [1024], replicated
- w_up: bfloat16 [1024, 4096], P(None, 'tp')
- w_down: bfloat16 [4096, 1024], P('tp')
Outputs:
- output: bfloat16 [16, 1024], P('dp')
All inputs are finite; a program needn't handle non-finite values.
Results may differ from a plain program's by a relative error of at most 0.0166655.
Values sent between devices are 32-bit elements.
A program may use at most 1 GiB of HBM per device.

v0:
```python
import jax
import jax.numpy as jnp
from jax import lax
from jax.sharding import PartitionSpec as P

EPS = 1e-6
MASKED = -1e30


def rms_norm(tensor, gain):
    wide = tensor.astype(jnp.float32)
    mean_sq = jnp.mean(wide * wide, axis=-1, keepdims=True)
    return (wide * lax.rsqrt(mean_sq + EPS) * gain.astype(jnp.float32)).astype(jnp.bfloat16)


def distance_to_position(by_distance, first_pos, lengths, width):
    padded = jnp.pad(by_distance, ((0, 0), (0, 0), (width, 0)))
    starts = lengths - first_pos + 1
    taken = jax.vmap(lambda row, begin: lax.dynamic_slice_in_dim(row, begin, width, axis=1))(padded, starts)
    return jnp.flip(taken, axis=2)


def solution(mesh):
    spec_rows = P('dp', None)
    spec_cache = P('dp', 'sp', 'tp', None)
    in_specs = (spec_rows, spec_cache, spec_cache, P('dp'), P('sp', 'tp', None), P('tp', None), P('tp', None), P(None), P(None, 'tp', None), P(None, 'tp', None), P(None, 'tp', None), P('tp', None, None), P(None), P(None, 'tp'), P('tp', None))
    out_specs = spec_rows

    def layer_step(hidden, k_cache, v_cache, lengths, rel_table, u_bias, w_bias, g_attn, w_query, w_key, w_value, w_out, g_mlp, w_up, w_down):
        seq_blk = k_cache.shape[1]
        head_dim = k_cache.shape[3]
        first_pos = lax.axis_index('sp') * seq_blk
        normed = rms_norm(hidden, g_attn)
        query_vec = jnp.einsum('do,ojf->djf', normed, w_query, preferred_element_type=jnp.float32).astype(jnp.bfloat16)
        key_new = jnp.einsum('do,ojf->djf', normed, w_key, preferred_element_type=jnp.float32).astype(jnp.bfloat16)
        value_new = jnp.einsum('do,ojf->djf', normed, w_value, preferred_element_type=jnp.float32).astype(jnp.bfloat16)
        positions = first_pos + jnp.arange(seq_blk)
        write_mask = (positions[None, :] == lengths[:, None])[:, :, None, None]
        k_updated = jnp.where(write_mask, key_new[:, None], k_cache)
        v_updated = jnp.where(write_mask, value_new[:, None], v_cache)
        q_content = (query_vec.astype(jnp.float32) + u_bias.astype(jnp.float32)).astype(jnp.bfloat16)
        q_position = (query_vec.astype(jnp.float32) + w_bias.astype(jnp.float32)).astype(jnp.bfloat16)
        content = jnp.einsum('bhd,bshd->bhs', q_content, k_updated, preferred_element_type=jnp.float32)
        rel_local = jnp.einsum('bhd,shd->bhs', q_position, rel_table, preferred_element_type=jnp.float32)
        rel_all = lax.all_gather(rel_local, 'sp', axis=2, tiled=True)
        relative = distance_to_position(rel_all, first_pos, lengths, seq_blk)
        valid = (positions[None, :] <= lengths[:, None])[:, None, :]
        scores = jnp.where(valid, (content + relative) * (head_dim ** -0.5), MASKED)
        local_max = jnp.max(scores, axis=2)
        weights = jnp.where(valid, jnp.exp(scores - local_max[:, :, None]), 0.0)
        local_sum = jnp.sum(weights, axis=2)
        partial_ctx = jnp.einsum('bhs,bshd->bhd', weights.astype(jnp.bfloat16), v_updated, preferred_element_type=jnp.float32)
        packed = jnp.concatenate([partial_ctx, local_max[:, :, None], local_sum[:, :, None]], axis=2)
        gathered = lax.all_gather(packed, 'sp', axis=0)
        block_ctx = gathered[:, :, :, :head_dim]
        block_max = gathered[:, :, :, head_dim]
        block_sum = gathered[:, :, :, head_dim + 1]
        global_max = jnp.max(block_max, axis=0)
        rescale = jnp.exp(block_max - global_max[None])
        total = jnp.sum(rescale * block_sum, axis=0)
        context = (jnp.sum(rescale[:, :, :, None] * block_ctx, axis=0) / total[:, :, None]).astype(jnp.bfloat16)
        attn_part = jnp.einsum('bhd,hdm->bm', context, w_out, preferred_element_type=jnp.float32)
        attn_out = lax.psum(attn_part, 'tp')
        resid_mid = (hidden.astype(jnp.float32) + attn_out).astype(jnp.bfloat16)
        normed_mlp = rms_norm(resid_mid, g_mlp)
        up_proj = jnp.dot(normed_mlp, w_up, preferred_element_type=jnp.float32)
        activated = jax.nn.gelu(up_proj, approximate=True).astype(jnp.bfloat16)
        down_part = jnp.dot(activated, w_down, preferred_element_type=jnp.float32)
        down_proj = lax.psum(down_part, 'tp')
        hidden_out = (resid_mid.astype(jnp.float32) + down_proj).astype(jnp.bfloat16)
        return hidden_out

    return jax.shard_map(layer_step, mesh=mesh, in_specs=in_specs, out_specs=out_specs, check_vma=False)
```

profile of v0, /device:TPU:0, one launch (start us, length us, event | category | flops | bytes accessed | tf_op | source)
XLA Modules:
  0.0 253.9 jit_solution(16610062051069842318)
XLA Ops:
  8.9 1.8 fusion.13
  10.7 4.2 %convolution_bitcast_fusion = f32[16,8,4096]{2,0,1:T(8,128)} fusion(bf16[4096,8,64]{0,2,1:T(8,128)(2,1)} %param.19, f32[16,8,64]{2,0,1:T(8,128)S(1)} %fusion.13, f32[8,64]{1,0:T(8,128)S(1)} %convert_element_type.70), kind=kOutput, calls=%fused_computation.11 | convolution fusion | flops 67125248 | bytes 6326272 | tf_op jit(solution)/shard_map/bhd,shd->bhs/dot_general | solution.py:44
  15.0 1.1 copy-done.2
  17.5 24.1 %fusion.2 = f32[16,8,1,4096]{3,2,1,0:T(1,128)} fusion(bf16[16,4096,8,64]{1,3,2,0:T(8,128)(2,1)} %param.16, pred[16,4096]{1,0:T(8,128)(4,1)S(1)} %get-tuple-element.59, bf16[16,8,64]{2,1,0:T(8,128)(2,1)S(1)} %copy.71, bf16[16,8,64,1]{2,0,1,3:T(8,128)(2,1)S(1)} %fusion.39), kind=kOutput, calls=%fused_computation.5 | convolution fusion | flops 100663296 | bytes 69304320 | tf_op jit(solution)/shard_map/bhd,bshd->bhs/dot_general | solution.py:43
  41.6 32.0 %all-gather.3.cloned.1.call-done = f32[16,8,16384]{2,0,1:T(8,128)} async-done(((f32[16,8,4096]{2,0,1:T(8,128)}), f32[16,8,16384]{2,0,1:T(8,128)}) %all-gather.3.cloned.1.call-update) | async-done | bytes 8388624 | tf_op jit(solution)/shard_map/all_gather | solution.py:45
  73.6 8.5 %pad.5 = f32[16,8,20480]{2,0,1:T(8,128)} pad(f32[16,8,16384]{2,0,1:T(8,128)} %all-gather.3.cloned.1.call-done, f32[]{:T(128)} %constant.17.clone.1), padding=0_0x0_0x4096_0 | pad | bytes 18874372 | tf_op jit(solution)/shard_map/jit(_pad)/pad | solution.py:17
  82.1 67.1 %while.2 = (s32[]{:T(128)}, f32[16,8,20480]{2,0,1:T(8,128)}, s32[16,3]{0,1:T(4,128)S(1)}, f32[16,8,4096]{2,1,0:T(8,128)}) while((s32[]{:T(128)}, f32[16,8,20480]{2,0,1:T(8,128)}, s32[16,3]{0,1:T(4,128)S(1)}, f32[16,8,4096]{2,1,0:T(8,128)}) %tuple.35), condition=%wide.while_cond.clone, body=%wide.while_body.sunk.clone | while | flops 2 | bytes 524405 | solution.py:19
  82.8 2.8 %constant_dynamic-slice_fusion.7 = f32[1,8,4096]{2,0,1:T(1,128)S(1)} fusion(f32[16,8,20480]{2,0,1:T(8,128)} %get-tuple-element.110, s32[]{:T(128)} %bitcast.57, s32[]{:T(128)} %bitcast.58), kind=kLoop, calls=%fused_computation.2.clone.1.clone | loop fusion | bytes 262152 | tf_op jit(solution)/shard_map/vmap()/gather
  86.9 2.8 %constant_dynamic-slice_fusion.7 = f32[1,8,4096]{2,0,1:T(1,128)S(1)} fusion(f32[16,8,20480]{2,0,1:T(8,128)} %get-tuple-element.110, s32[]{:T(128)} %bitcast.57, s32[]{:T(128)} %bitcast.58), kind=kLoop, calls=%fused_computation.2.clone.1.clone | loop fusion | bytes 262152 | tf_op jit(solution)/shard_map/vmap()/gather
  91.1 2.8 %constant_dynamic-slice_fusion.7 = f32[1,8,4096]{2,0,1:T(1,128)S(1)} fusion(f32[16,8,20480]{2,0,1:T(8,128)} %get-tuple-element.110, s32[]{:T(128)} %bitcast.57, s32[]{:T(128)} %bitcast.58), kind=kLoop, calls=%fused_computation.2.clone.1.clone | loop fusion | bytes 262152 | tf_op jit(solution)/shard_map/vmap()/gather
  95.3 2.8 %constant_dynamic-slice_fusion.7 = f32[1,8,4096]{2,0,1:T(1,128)S(1)} fusion(f32[16,8,20480]{2,0,1:T(8,128)} %get-tuple-element.110, s32[]{:T(128)} %bitcast.57, s32[]{:T(128)} %bitcast.58), kind=kLoop, calls=%fused_computation.2.clone.1.clone | loop fusion | bytes 262152 | tf_op jit(solution)/shard_map/vmap()/gather
  99.5 2.8 %constant_dynamic-slice_fusion.7 = f32[1,8,4096]{2,0,1:T(1,128)S(1)} fusion(f32[16,8,20480]{2,0,1:T(8,128)} %get-tuple-element.110, s32[]{:T(128)} %bitcast.57, s32[]{:T(128)} %bitcast.58), kind=kLoop, calls=%fused_computation.2.clone.1.clone | loop fusion | bytes 262152 | tf_op jit(solution)/shard_map/vmap()/gather
  103.7 2.8 %constant_dynamic-slice_fusion.7 = f32[1,8,4096]{2,0,1:T(1,128)S(1)} fusion(f32[16,8,20480]{2,0,1:T(8,128)} %get-tuple-element.110, s32[]{:T(128)} %bitcast.57, s32[]{:T(128)} %bitcast.58), kind=kLoop, calls=%fused_computation.2.clone.1.clone | loop fusion | bytes 262152 | tf_op jit(solution)/shard_map/vmap()/gather
  107.9 2.8 %constant_dynamic-slice_fusion.7 = f32[1,8,4096]{2,0,1:T(1,128)S(1)} fusion(f32[16,8,20480]{2,0,1:T(8,128)} %get-tuple-element.110, s32[]{:T(128)} %bitcast.57, s32[]{:T(128)} %bitcast.58), kind=kLoop, calls=%fused_computation.2.clone.1.clone | loop fusion | bytes 262152 | tf_op jit(solution)/shard_map/vmap()/gather
  112.1 2.8 %constant_dynamic-slice_fusion.7 = f32[1,8,4096]{2,0,1:T(1,128)S(1)} fusion(f32[16,8,20480]{2,0,1:T(8,128)} %get-tuple-element.110, s32[]{:T(128)} %bitcast.57, s32[]{:T(128)} %bitcast.58), kind=kLoop, calls=%fused_computation.2.clone.1.clone | loop fusion | bytes 262152 | tf_op jit(solution)/shard_map/vmap()/gather
  116.3 2.8 %constant_dynamic-slice_fusion.7 = f32[1,8,4096]{2,0,1:T(1,128)S(1)} fusion(f32[16,8,20480]{2,0,1:T(8,128)} %get-tuple-element.110, s32[]{:T(128)} %bitcast.57, s32[]{:T(128)} %bitcast.58), kind=kLoop, calls=%fused_computation.2.clone.1.clone | loop fusion | bytes 262152 | tf_op jit(solution)/shard_map/vmap()/gather
  120.5 2.8 %constant_dynamic-slice_fusion.7 = f32[1,8,4096]{2,0,1:T(1,128)S(1)} fusion(f32[16,8,20480]{2,0,1:T(8,128)} %get-tuple-element.110, s32[]{:T(128)} %bitcast.57, s32[]{:T(128)} %bitcast.58), kind=kLoop, calls=%fused_computation.2.clone.1.clone | loop fusion | bytes 262152 | tf_op jit(solution)/shard_map/vmap()/gather
  124.7 2.8 %constant_dynamic-slice_fusion.7 = f32[1,8,4096]{2,0,1:T(1,128)S(1)} fusion(f32[16,8,20480]{2,0,1:T(8,128)} %get-tuple-element.110, s32[]{:T(128)} %bitcast.57, s32[]{:T(128)} %bitcast.58), kind=kLoop, calls=%fused_computation.2.clone.1.clone | loop fusion | bytes 262152 | tf_op jit(solution)/shard_map/vmap()/gather
  128.9 2.8 %constant_dynamic-slice_fusion.7 = f32[1,8,4096]{2,0,1:T(1,128)S(1)} fusion(f32[16,8,20480]{2,0,1:T(8,128)} %get-tuple-element.110, s32[]{:T(128)} %bitcast.57, s32[]{:T(128)} %bitcast.58), kind=kLoop, calls=%fused_computation.2.clone.1.clone | loop fusion | bytes 262152 | tf_op jit(solution)/shard_map/vmap()/gather
  133.1 2.8 %constant_dynamic-slice_fusion.7 = f32[1,8,4096]{2,0,1:T(1,128)S(1)} fusion(f32[16,8,20480]{2,0,1:T(8,128)} %get-tuple-element.110, s32[]{:T(128)} %bitcast.57, s32[]{:T(128)} %bitcast.58), kind=kLoop, calls=%fused_computation.2.clone.1.clone | loop fusion | bytes 262152 | tf_op jit(solution)/shard_map/vmap()/gather
  137.3 2.8 %constant_dynamic-slice_fusion.7 = f32[1,8,4096]{2,0,1:T(1,128)S(1)} fusion(f32[16,8,20480]{2,0,1:T(8,128)} %get-tuple-element.110, s32[]{:T(128)} %bitcast.57, s32[]{:T(128)} %bitcast.58), kind=kLoop, calls=%fused_computation.2.clone.1.clone | loop fusion | bytes 262152 | tf_op jit(solution)/shard_map/vmap()/gather
  141.4 2.8 %constant_dynamic-slice_fusion.7 = f32[1,8,4096]{2,0,1:T(1,128)S(1)} fusion(f32[16,8,20480]{2,0,1:T(8,128)} %get-tuple-element.110, s32[]{:T(128)} %bitcast.57, s32[]{:T(128)} %bitcast.58), kind=kLoop, calls=%fused_computation.2.clone.1.clone | loop fusion | bytes 262152 | tf_op jit(solution)/shard_map/vmap()/gather
  145.6 2.8 %constant_dynamic-slice_fusion.7 = f32[1,8,4096]{2,0,1:T(1,128)S(1)} fusion(f32[16,8,20480]{2,0,1:T(8,128)} %get-tuple-element.110, s32[]{:T(128)} %bitcast.57, s32[]{:T(128)} %bitcast.58), kind=kLoop, calls=%fused_computation.2.clone.1.clone | loop fusion | bytes 262152 | tf_op jit(solution)/shard_map/vmap()/gather
  149.2 14.9 %rev.4 = f32[16,8,4096]{2,1,0:T(8,128)S(1)} reverse(f32[16,8,4096]{2,1,0:T(8,128)} %get-tuple-element.12), dimensions={2} | reverse | bytes 4194304 | tf_op jit(solution)/shard_map/jit(_flip)/rev | solution.py:20
  164.1 3.3 %fusion.63 = f32[16,8]{1,0:T(8,128)S(1)} fusion(f32[16,8,4096]{2,1,0:T(8,128)S(1)} %rev.4, f32[16,8,1,4096]{3,2,1,0:T(1,128)} %fusion.2, pred[16,4096]{1,0:T(8,128)(4,1)S(1)} %get-tuple-element.58), kind=kLoop, calls=%fused_computation.85 | loop fusion | flops 2097024 | bytes 4260352 | tf_op jit(solution)/shard_map/reduce_max | solution.py:49
  167.4 2.8 %fusion.14 = (bf16[16,8,4096,1]{2,1,0,3:T(8,128)(2,1)}, f32[16,8]{1,0:T(8,128)S(1)}) fusion(f32[16,8]{1,0:T(8,128)S(1)} %fusion.63, pred[16,4096]{1,0:T(8,128)(4,1)S(1)} %get-tuple-element.58, f32[16,8,4096]{2,1,0:T(8,128)S(1)} %rev.4, f32[16,8,1,4096]{3,2,1,0:T(1,128)S(1)} %copy-done.1), kind=kLoop, calls=%fused_computation.24 | loop fusion | flops 3669888 | bytes 5309440 | tf_op jit(solution)/shard_map/convert_element_type | solution.py:52
  170.6 26.8 %fusion = f32[16,8,1,64]{3,2,1,0:T(1,128)S(1)} fusion(bf16[16,4096,8,64]{1,3,2,0:T(8,128)(2,1)} %param.17, pred[16,4096]{1,0:T(8,128)(4,1)S(1)} %get-tuple-element.59, bf16[16,8,64]{2,1,0:T(8,128)(2,1)S(1)} %copy.73, bf16[16,8,4096,1]{2,1,0,3:T(8,128)(2,1)} %get-tuple-element.53), kind=kOutput, calls=%fused_computation.3 | convolution fusion | flops 100663296 | bytes 68272128 | tf_op jit(solution)/shard_map/bhs,bshd->bhd/dot_general | solution.py:52
  197.5 7.8 %all-gather = f32[64,8,66]{2,1,0:T(8,128)S(1)} all-gather(f32[16,8,66]{2,1,0:T(8,128)S(1)} %pad_maximum_fusion), channel_id=2, replica_groups=mesh['dp'=1,'tp'=2,'sp'=4] {'sp'}, dimensions={0}, use_global_device_ids=true | all-gather | bytes 168960 | tf_op jit(solution)/shard_map/all_gather | solution.py:54
  207.6 16.5 %all-reduce.5.cloned.1.call-done = f32[16,1024]{1,0:T(8,128)} async-done(((f32[16,1024]{1,0:T(8,128)}), f32[16,1024]{1,0:T(8,128)}) %all-reduce.5.cloned.1.call-update) | async-done | bytes 65552 | tf_op jit(solution)/shard_map/psum | solution.py:63
  225.1 5.3 %fusion.32 = f32[16,1024]{1,0:T(8,128)} fusion(bf16[2048,1024]{1,0:T(8,128)(2,1)} %param.29, bf16[1024,2048]{1,0:T(8,128)(2,1)} %param.28, bf16[16,1024]{1,0:T(8,128)(2,1)S(1)} %get-tuple-element.50, f32[1024]{0:T(1024)S(1)} %convert_element_type.77, f32[16]{0:T(128)S(1)} %add_rsqrt_fusion), kind=kOutput, calls=%fused_computation.52 | convolution fusion | flops 134578176 | bytes 8491072 | tf_op jit(solution)/shard_map/dot_general | solution.py:68
  230.5 15.5 %all-reduce.7.cloned.1.call-done = f32[16,1024]{1,0:T(8,128)} async-done(((f32[16,1024]{1,0:T(8,128)}), f32[16,1024]{1,0:T(8,128)}) %all-reduce.7.cloned.1.call-update) | async-done | bytes 65552 | tf_op jit(solution)/shard_map/psum | solution.py:69
  245.9 1.5 fusion.31
  (102 shorter events, 29.6 us)
Async XLA Ops:
  6.5 200.1 %copy-start = (bf16[8,64,1024]{2,1,0:T(8,128)(2,1)S(1)}, bf16[8,64,1024]{2,1,0:T(8,128)(2,1)}, u32[]{:S(2)}) copy-start(bf16[8,64,1024]{2,1,0:T(8,128)(2,1)} %param.26) | copy-start | bytes 3145732
  6.5 67.1 %all-gather.3.cloned.1.call-start = ((), (), s32[]{:S(2)}) async-start(), calls=%async_computation | async-start | bytes 10485760 | tf_op jit(solution)/shard_map/all_gather | solution.py:45
  10.7 4.3 %copy-start.4 = (bf16[16,1024]{1,0:T(8,128)(2,1)S(1)}, bf16[16,1024]{1,0:T(8,128)(2,1)}, u32[]{:S(2)}) copy-start(bf16[16,1024]{1,0:T(8,128)(2,1)} %param.15) | copy-start | bytes 98308
  14.9 1.2 copy-start.2
  14.9 1.8 copy-start.5
  14.9 1.8 copy-start.3
  14.9 2.4 copy-start.7
  14.9 209.2 %all-reduce.5.cloned.1.call-start = ((), (), s32[]{:S(2)}) async-start(), calls=%async_computation.1 | async-start | bytes 131072 | tf_op jit(solution)/shard_map/psum | solution.py:63
  164.1 3.3 %copy-start.1 = (f32[16,8,1,4096]{3,2,1,0:T(1,128)S(1)}, f32[16,8,1,4096]{3,2,1,0:T(1,128)}, u32[]{:S(2)}) copy-start(f32[16,8,1,4096]{3,2,1,0:T(1,128)} %fusion.2) | copy-start | bytes 6291460
  197.4 10.2 %copy-start.6 = (bf16[1024]{0:T(1024)(128)(2,1)S(1)}, bf16[1024]{0:T(1024)(128)(2,1)}, u32[]{:S(2)}) copy-start(bf16[1024]{0:T(1024)(128)(2,1)} %param.27) | copy-start | bytes 6148
  207.5 38.4 %all-reduce.7.cloned.1.call-start = ((), (), s32[]{:S(2)}) async-start(), calls=%async_computation.2 | async-start | bytes 131072 | tf_op jit(solution)/shard_map/psum | solution.py:69
Sparse Core Ops, SparseCore 0:
  15.1 58.5 all-gather.2
  207.7 16.4 all-reduce.4
  230.6 15.2 all-reduce.6
where the time goes:
time: 256 us; the launch traced here: 254 us
  local copies, waits for them, and re-layouts  92.7 us (36%)
  matrix products  64.2 us (25%)
  waiting for transfers between devices  64.1 us (25%)
  between operations  13.3 us (5%)
  other arithmetic  11.8 us (5%)
  blocking collectives  7.8 us (3%)
    gather x64, local copies, waits for them, and re-layouts  67 us
    all_gather x1, waiting for transfers between devices, layer_step(): rel_all = lax.all_gather(rel_local, 'sp', axis=2, tiled=True)  32 us
    dot_general x1, matrix products, layer_step(): jnp.einsum('bhs,bshd->bhd', weights.astype(jnp.bfloat16), v_updated, pref...  26.8 us
    dot_general x1, matrix products, layer_step(): jnp.einsum('bhd,bshd->bhs', q_content, k_updated, preferred_element_type=...  24.1 us
    psum x1, waiting for transfers between devices, layer_step(): attn_out = lax.psum(attn_part, 'tp')  16.5 us
    psum x1, waiting for transfers between devices, layer_step(): down_proj = lax.psum(down_part, 'tp')  15.5 us
    rev x1, local copies, waits for them, and re-layouts, distance_to_position(): return jnp.flip(taken, axis=2)  14.9 us
    pad x1, local copies, waits for them, and re-layouts, distance_to_position(): padded = jnp.pad(by_distance, ((0, 0), (0, 0), (width, 0)))  8.47 us
  transfers between devices with their start and end apart: 3, of which 3 were waited for; matrix products, arithmetic and copies ran while one was open for 10% of the time, Pallas kernels for 0%

commit v1 on v0

v1 whole, which is shorter than its diff:
```python
import functools

import jax
import jax.numpy as jnp
from jax import lax
from jax.experimental import pallas as pl
from jax.experimental.pallas import tpu as pltpu
from jax.sharding import PartitionSpec as P

EPS = 1e-6
MASKED = -1e30
MESH = pl.DeviceIdType.MESH
F32 = jnp.float32
BF16 = jnp.bfloat16
NT = (((1,), (1,)), ((), ()))
NS = 10


def rms(x, gain):
    mean_sq = jnp.mean(x * x, axis=-1, keepdims=True)
    return (x * lax.rsqrt(mean_sq + EPS) * gain).astype(BF16)


def kernel(hid_ref, k_hbm, v_hbm, len_ref, r_hbm, u_ref, w_ref, ga_ref, wq_hbm, wk_hbm, wv_hbm, wo_hbm, gm_ref, wu_hbm, wd_hbm,
           out_ref,
           ring, rel_own, rel_par, rel_cro, rel_dia, content, wo, wu, wd, qc_bd, k_new, v_new, rows_acc, part, asend, arecv, dsend, drecv,
           ring_sem, wt_sem, par_sem, cro_send, cro_recv, dia_send, dia_recv, part_send, part_recv, ex_sem):
    nb, nh, width = content.shape
    feat = k_hbm.shape[1]
    hd = feat // nh
    sp = lax.axis_index("sp")
    tp = lax.axis_index("tp")
    chip = sp // 2
    core = lax.rem(sp, 2)
    partner = chip * 2 + (1 - core)
    cross = (1 - chip) * 2 + core
    diag = (1 - chip) * 2 + (1 - core)

    barrier = pltpu.get_barrier_semaphore()
    for peer in (partner, cross, diag):
        pl.semaphore_signal(barrier, inc=1, device_id={"sp": peer}, device_id_type=MESH)
    pl.semaphore_signal(barrier, inc=1, device_id={"tp": 1 - tp}, device_id_type=MESH)

    def load(src, dst, sem):
        return pltpu.make_async_copy(src, dst, sem)

    def k_load(b):
        return load(k_hbm.at[b], ring.at[lax.rem(b, NS)], ring_sem.at[lax.rem(b, NS)])

    def v_load(b):
        slot = lax.rem(b + nb, NS)
        return load(v_hbm.at[b], ring.at[slot], ring_sem.at[slot])

    wdt = wq_hbm.shape[1]
    stage = ring.at[NS - 2]
    r_copy = load(r_hbm, ring.at[NS - 1], ring_sem.at[NS - 1])
    wq_copy = load(wq_hbm, stage.at[:, pl.ds(0, wdt)], wt_sem.at[0])
    wk_copy = load(wk_hbm, stage.at[:, pl.ds(wdt, wdt)], wt_sem.at[1])
    wv_copy = load(wv_hbm, stage.at[:, pl.ds(2 * wdt, wdt)], wt_sem.at[2])
    wo_copy = load(wo_hbm, wo, wt_sem.at[3])
    wu_copy = load(wu_hbm, wu, wt_sem.at[4])
    wd_copy = load(wd_hbm, wd, wt_sem.at[5])
    wq_copy.start()
    r_copy.start()
    wk_copy.start()
    wv_copy.start()
    for b in range(NS - 2):
        k_load(b).start()

    hidden = hid_ref[...].astype(F32)
    normed = rms(hidden, ga_ref[...].astype(F32))

    head_of_row = lax.broadcasted_iota(jnp.int32, (nh, feat), 0)
    head_of_col = lax.broadcasted_iota(jnp.int32, (nh, feat), 1) // hd
    diag_mask = head_of_row == head_of_col
    spread_row = lax.broadcasted_iota(jnp.int32, (hd, feat), 0)
    spread_col = lax.rem(lax.broadcasted_iota(jnp.int32, (hd, feat), 1), hd)
    spread = (spread_row == spread_col).astype(BF16)
    u_wide = jnp.dot(u_ref[...], spread, preferred_element_type=F32)
    w_wide = jnp.dot(w_ref[...], spread, preferred_element_type=F32)

    wq_copy.wait()
    query = lax.dot_general(normed, stage[:, pl.ds(0, wdt)], NT, preferred_element_type=F32).astype(BF16).astype(F32)
    zero_rows = jnp.zeros((nh, feat), F32)
    pos_rows = []
    for b in range(nb):
        row = query[b:b + 1, :]
        qc = jnp.where(diag_mask, row + u_wide, 0.0)
        qc_bd[b] = jnp.concatenate([qc, zero_rows], axis=0).astype(BF16)
        pos_rows.append(jnp.where(diag_mask, row + w_wide, 0.0))
    q_pos = jnp.concatenate(pos_rows, axis=0).astype(BF16)

    r_copy.wait()
    step = 1024
    for c in range(width // step):
        cols = pl.ds(c * step, step)
        prod = jnp.dot(q_pos, ring[NS - 1, :, cols], preferred_element_type=F32)
        rel_own[:, :, cols] = prod.reshape(nb, nh, step)
    pl.semaphore_wait(barrier, 4)

    par_copy = pltpu.make_async_remote_copy(src_ref=rel_own, dst_ref=rel_par, send_sem=par_sem.at[0], recv_sem=par_sem.at[1],
                                            device_id={"sp": partner}, device_id_type=MESH)

    def cross_copy(i):
        return pltpu.make_async_remote_copy(src_ref=rel_own.at[i], dst_ref=rel_cro.at[i], send_sem=cro_send.at[i], recv_sem=cro_recv.at[i],
                                            device_id={"sp": cross}, device_id_type=MESH)

    def forward_copy(i):
        return pltpu.make_async_remote_copy(src_ref=rel_cro.at[i], dst_ref=rel_dia.at[i], send_sem=dia_send.at[i], recv_sem=dia_recv.at[i],
                                            device_id={"sp": partner}, device_id_type=MESH)

    par_copy.start()
    for i in range(nb):
        cross_copy(i).start()

    wk_copy.wait()
    k_new[...] = lax.dot_general(normed, stage[:, pl.ds(wdt, wdt)], NT, preferred_element_type=F32).astype(BF16).astype(F32)
    wv_copy.wait()
    v_new[...] = lax.dot_general(normed, stage[:, pl.ds(2 * wdt, wdt)], NT, preferred_element_type=F32).astype(BF16).astype(F32)
    for b in range(NS - 2, NS):
        k_load(b).start()

    @pl.loop(0, nb)
    def _(b):
        k_load(b).wait()
        content[b] = jnp.dot(qc_bd[b], ring[lax.rem(b, NS)], preferred_element_type=F32)[:nh]

        @pl.when(b < nb - NS)
        def _():
            k_load(b + NS).start()

        @pl.when(b >= nb - NS)
        def _():
            v_load(b + NS - nb).start()

    wo_copy.start()
    wu_copy.start()
    wd_copy.start()
    par_copy.wait()

    lane = lax.broadcasted_iota(jnp.int32, (nh, width), 1)
    back = 127 - lax.broadcasted_iota(jnp.int32, (nh, 128), 1)
    stat_lane = lax.broadcasted_iota(jnp.int32, (nh, 128), 1)
    stat_row = lax.broadcasted_iota(jnp.int32, (nh, 128), 0)

    def attend(b):
        length = len_ref[b]
        high = length // width
        low = length - high * width
        first = high - sp
        upper = lane <= low
        comb = jnp.zeros((nh, width), F32)
        for block, rows in ((sp, rel_own), (partner, rel_par), (cross, rel_cro), (diag, rel_dia)):
            want = jnp.where(upper, first, first - 1) == block
            comb = jnp.where(want, rows[b], comb)
        pieces = [jnp.take_along_axis(comb[:, 128 * c:128 * c + 128], back, axis=1) for c in range(width // 128)]
        relative = pltpu.roll(jnp.concatenate(pieces[::-1], axis=1), lax.rem(low + 1, width), axis=1)
        here = length - sp * width
        valid = lane <= here
        is_new = lane == here
        q_rows = qc_bd[b][:nh].astype(F32)
        s_new = jnp.sum(q_rows * k_new[pl.ds(b, 1), :], axis=1, keepdims=True)
        scores = jnp.where(is_new, s_new, content[b]) + relative
        scores = jnp.where(valid, scores * (hd ** -0.5), MASKED)
        top = jnp.max(scores, axis=1, keepdims=True)
        weights = jnp.where(valid, jnp.exp(scores - top), 0.0)
        total = jnp.sum(weights, axis=1, keepdims=True)
        p_new = jnp.sum(jnp.where(is_new, weights, 0.0), axis=1, keepdims=True).astype(BF16).astype(F32)
        cached = jnp.where(is_new, 0.0, weights).astype(BF16)
        slot = lax.rem(b + nb, NS)
        v_load(b).wait()
        mixed = lax.dot_general(cached, ring[slot], NT, preferred_element_type=F32)
        mixed = mixed + p_new * v_new[pl.ds(b, 1), :]
        rows_acc[b, :, pl.ds(0, feat)] = jnp.sum(jnp.where(diag_mask, mixed, 0.0), axis=0, keepdims=True)
        stats = jnp.where(stat_lane == stat_row, top, jnp.where(stat_lane == stat_row + nh, total, 0.0))
        rows_acc[b, :, pl.ds(feat, 128)] = jnp.sum(stats, axis=0, keepdims=True)

        @pl.when(b < nb - NS)
        def _():
            v_load(b + NS).start()

    @pl.loop(0, nb + 1)
    def _(i):
        @pl.when(i < nb)
        def _():
            cross_copy(i).wait()
            forward_copy(i).start()

        @pl.when(i >= 1)
        def _():
            forward_copy(i - 1).wait()
            attend(i - 1)

    for b in range(nb):
        part[0, b:b + 1, :] = rows_acc[b]
    part_copies = []
    for j, peer in ((1, partner), (2, cross), (3, diag)):
        part_copies.append(pltpu.make_async_remote_copy(src_ref=part.at[0], dst_ref=part.at[j], send_sem=part_send.at[j], recv_sem=part_recv.at[j],
                                                        device_id={"sp": peer}, device_id_type=MESH))
    for copy in part_copies:
        copy.start()
    for copy in part_copies:
        copy.wait()

    blocks = []
    for s in range(4):
        j = lax.rem(chip + s // 2, 2) * 2 + lax.rem(core + s % 2, 2)
        blocks.append(part[j])
    tops = [x[:, feat:] for x in blocks]
    top_all = functools.reduce(jnp.maximum, tops)
    scale = [jnp.exp(t - top_all) for t in tops]
    total = sum(s * pltpu.roll(t, 128 - nh, axis=1) for s, t in zip(scale, tops))
    lane_head = lax.broadcasted_iota(jnp.int32, (nb, 128), 1) // hd
    context = jnp.zeros((nb, feat), F32)
    for s, x in zip(scale, blocks):
        factor = s / total
        wide = jnp.concatenate([jnp.take_along_axis(factor, lane_head + c * (128 // hd), axis=1) for c in range(feat // 128)], axis=1)
        context = context + wide * x[:, :feat]

    def exchange(send, recv, j):
        return pltpu.make_async_remote_copy(src_ref=send, dst_ref=recv, send_sem=ex_sem.at[2 * j], recv_sem=ex_sem.at[2 * j + 1],
                                            device_id={"tp": 1 - tp}, device_id_type=MESH)

    wo_copy.wait()
    attn = jnp.dot(context.astype(BF16), wo[...], preferred_element_type=F32)
    asend[...] = attn
    swap = exchange(asend, arecv, 0)
    swap.start()
    swap.wait()
    middle = (hidden + (attn + arecv[...])).astype(BF16).astype(F32)
    normed_mlp = rms(middle, gm_ref[...].astype(F32))
    wu_copy.wait()
    up = jnp.dot(normed_mlp, wu[...], preferred_element_type=F32)
    act = jax.nn.gelu(up, approximate=True).astype(BF16)
    wd_copy.wait()
    down = jnp.dot(act, wd[...], preferred_element_type=F32)
    dsend[...] = down
    swap = exchange(dsend, drecv, 1)
    swap.start()
    swap.wait()
    out_ref[...] = (middle + (down + drecv[...])).astype(BF16)


def solution(mesh):
    spec_cache = P('dp', 'sp', 'tp', None)
    in_specs = (P('dp', None), spec_cache, spec_cache, P('dp'), P('sp', 'tp', None), P('tp', None), P('tp', None), P(None), P(None, 'tp', None), P(None, 'tp', None), P(None, 'tp', None), P('tp', None, None), P(None), P(None, 'tp'), P('tp', None))

    def layer_step(hidden, k_cache, v_cache, lengths, rel_table, u_bias, w_bias, g_attn, w_query, w_key, w_value, w_out, g_mlp, w_up, w_down):
        nb, width, nh, hd = k_cache.shape
        feat = nh * hd
        model = hidden.shape[1]
        k_t = k_cache.transpose(0, 2, 3, 1).reshape(nb, feat, width)
        v_t = v_cache.transpose(0, 2, 3, 1).reshape(nb, feat, width)
        r_t = rel_table.transpose(1, 2, 0).reshape(feat, width)
        proj = [w.transpose(1, 2, 0).reshape(feat, model) for w in (w_query, w_key, w_value)]
        vmem = pl.BlockSpec(memory_space=pltpu.VMEM)
        hbm = pl.BlockSpec(memory_space=pl.ANY)
        smem = pl.BlockSpec(memory_space=pltpu.SMEM)
        dma = pltpu.SemaphoreType.DMA
        return pl.pallas_call(
            kernel,
            out_shape=jax.ShapeDtypeStruct((nb, model), BF16),
            in_specs=[vmem, hbm, hbm, smem, hbm, vmem, vmem, vmem, hbm, hbm, hbm, hbm, vmem, hbm, hbm],
            out_specs=vmem,
            scratch_shapes=[
                pltpu.VMEM((NS, feat, width), BF16),
                pltpu.VMEM((nb, nh, width), F32),
                pltpu.VMEM((nb, nh, width), F32),
                pltpu.VMEM((nb, nh, width), F32),
                pltpu.VMEM((nb, nh, width), F32),
                pltpu.VMEM((nb, nh, width), F32),
                pltpu.VMEM((feat, model), BF16),
                pltpu.VMEM(w_up.shape, BF16),
                pltpu.VMEM(w_down.shape, BF16),
                pltpu.VMEM((nb, 16, feat), BF16),
                pltpu.VMEM((nb, feat), F32),
                pltpu.VMEM((nb, feat), F32),
                pltpu.VMEM((nb, 1, feat + 128), F32),
                pltpu.VMEM((4, nb, feat + 128), F32),
                pltpu.VMEM((nb, model), F32),
                pltpu.VMEM((nb, model), F32),
                pltpu.VMEM((nb, model), F32),
                pltpu.VMEM((nb, model), F32),
                dma((NS,)), dma((6,)), dma((2,)), dma((nb,)), dma((nb,)), dma((nb,)), dma((nb,)), dma((4,)), dma((4,)), dma((4,)),
            ],
            compiler_params=pltpu.CompilerParams(collective_id=0, has_side_effects=True, vmem_limit_bytes=67043328),
        )(hidden, k_t, v_t, lengths, r_t, u_bias, w_bias, g_attn[None], *proj, w_out.reshape(feat, model), g_mlp[None], w_up, w_down)

    return jax.shard_map(layer_step, mesh=mesh, in_specs=in_specs, out_specs=P('dp', None), check_vma=False)
```

time: 256 us -> 72.7 us (0.28)
  local copies, waits for them, and re-layouts: 92.7 us -> 3.92 us
  Pallas kernels: 0 us -> 68.5 us
  matrix products: 64.2 us -> 0 us
  waiting for transfers between devices: 64.1 us -> 0 us
  between operations: 13.3 us -> 0.01 us
  other arithmetic: 11.8 us -> 0 us
  blocking collectives: 7.8 us -> 0 us
    pallas_call x0 -> x1, Pallas kernels: none -> 68.5 us  [layer_step(): pl.pallas_call(kernel, out_shape=jax.ShapeDtypeStruct((nb, model), BF16),...]
    gather x64 -> x0, local copies, waits for them, and re-layouts: 67 us -> none
    dot_general x8 -> x0, matrix products: 64.2 us -> none  [the longest x1 26.8 us: layer_step(): jnp.einsum('bhs,bshd->bhd', weights.astype(jnp.bfloat16), v_updated, pref...]
    all_gather x1 -> x0, waiting for transfers between devices: 32 us -> none  [layer_step(): rel_all = lax.all_gather(rel_local, 'sp', axis=2, tiled=True)]
    psum x2 -> x0, waiting for transfers between devices: 32 us -> none  [the longest x1 16.5 us: layer_step(): attn_out = lax.psum(attn_part, 'tp')]
    rev x1 -> x0, local copies, waits for them, and re-layouts: 14.9 us -> none  [distance_to_position(): return jnp.flip(taken, axis=2)]
    pad x1 -> x0, local copies, waits for them, and re-layouts: 8.47 us -> none  [distance_to_position(): padded = jnp.pad(by_distance, ((0, 0), (0, 0), (width, 0)))]
    all_gather x1 -> x0, blocking collectives: 7.8 us -> none  [layer_step(): gathered = lax.all_gather(packed, 'sp', axis=0)]
  transfers between devices with their start and end apart: 3 -> 0, of which waited for: 3 -> 0; matrix products, arithmetic and copies ran while one was open for 10% -> 0% of each run, Pallas kernels for 0% -> 0%
where the time goes in v1:
time: 72.7 us; the launch traced here: 72.5 us
  Pallas kernels  68.5 us (94%)
  local copies, waits for them, and re-layouts  3.92 us (5%)
    pallas_call x1, Pallas kernels, layer_step(): pl.pallas_call(kernel, out_shape=jax.ShapeDtypeStruct((nb, model), BF16),...  68.5 us

profile of v1, /device:TPU:0, one launch (start us, length us, event | category | flops | bytes accessed | tf_op | source)
XLA Modules:
  0.0 72.5 jit_solution(15649166440948963414)
XLA Ops:
  0.0 1.3 %broadcast_in_dim.6.ga_ref = bf16[1,1024]{1,0:T(2,128)(2,1)} reshape(bf16[1024]{0:T(1024)(128)(2,1)} %param.22) | data formatting | bytes 4096 | tf_op jit(solution)/shard_map/broadcast_in_dim | solution.py:287
  1.3 1.3 %broadcast_in_dim.7.gm_ref = bf16[1,1024]{1,0:T(2,128)(2,1)} reshape(bf16[1024]{0:T(1024)(128)(2,1)} %param.27) | data formatting | bytes 4096 | tf_op jit(solution)/shard_map/broadcast_in_dim | solution.py:287
  2.5 68.5 %shard_map.145 = bf16[16,1024]{1,0:T(8,128)(2,1)} custom-call(bf16[16,1024]{1,0:T(8,128)(2,1)} %hid_ref.1, bf16[16,512,4096]{2,1,0:T(8,128)(2,1)} %bitcast.1.k_hbm, bf16[16,512,4096]{2,1,0:T(8,128)(2,1)} %bitcast.3.v_hbm, s32[16]{0:T(128)} %len_ref.1, bf16[512,4096]{1,0:T(8,128)(2,1)} %bitcast.19, bf16[8,64]{1,0:T(8,128)(2,1)} %u_ref.1, ...), custom_call_target="tpu_custom_call" | custom-call | tf_op jit(solution)/shard_map/pallas_call | solution.py:260
  71.1 1.4 %copy.17 = bf16[16,1024]{1,0:T(8,128)(2,1)} copy(bf16[16,1024]{1,0:T(8,128)(2,1)} %shard_map.145) | data formatting | bytes 65536

commit v2 on v1

--- a/solution.py
+++ b/solution.py
@@ -14,6 +14,8 @@
 BF16 = jnp.bfloat16
 NT = (((1,), (1,)), ((), ()))
 NS = 10
+GROUP = 4
+STAGES = 4
 
 
 def rms(x, gain):
@@ -21,13 +23,17 @@
     return (x * lax.rsqrt(mean_sq + EPS) * gain).astype(BF16)
 
 
-def kernel(hid_ref, k_hbm, v_hbm, len_ref, r_hbm, u_ref, w_ref, ga_ref, wq_hbm, wk_hbm, wv_hbm, wo_hbm, gm_ref, wu_hbm, wd_hbm,
+def kernel(caps, hid_hbm, k_hbm, v_hbm, len_hbm, r_hbm, u_hbm, w_hbm, ga_hbm, wq_hbm, wk_hbm, wv_hbm, wo_hbm, gm_hbm, wu_hbm, wd_hbm,
            out_ref,
-           ring, rel_own, rel_par, rel_cro, rel_dia, content, wo, wu, wd, qc_bd, k_new, v_new, rows_acc, part, asend, arecv, dsend, drecv,
-           ring_sem, wt_sem, par_sem, cro_send, cro_recv, dia_send, dia_recv, part_send, part_recv, ex_sem):
+           hid_ref, len_ref, u_ref, w_ref, ga_ref, gm_ref, ring, rel_own, rel_par, content, probs, p_extra, wo, wu, wd, qc_bd, k_new, v_new, rows_acc, part, asend, arecv, dsend, drecv,
+           ring_sem, wt_sem, r_sem, par_sem, cro_send, cro_recv, dia_send, dia_recv, part_send, part_recv, ex_sem, table, *far_refs):
     nb, nh, width = content.shape
     feat = k_hbm.shape[1]
     hd = feat // nh
+    even, odd = caps
+    compact = even[-1] < nb
+    rel_cro, rel_dia = far_refs[:STAGES], far_refs[STAGES:2 * STAGES]
+    rel_send = far_refs[-1] if compact else rel_own
     sp = lax.axis_index("sp")
     tp = lax.axis_index("tp")
     chip = sp // 2
@@ -36,6 +42,15 @@
     cross = (1 - chip) * 2 + core
     diag = (1 - chip) * 2 + (1 - core)
 
+    def by_core(c, a, b):
+        return a + (b - a) * c
+
+    def size(g, c):
+        return by_core(c, even[g + 1] - even[g], odd[g + 1] - odd[g])
+
+    def begin(g, c):
+        return by_core(c, even[g], odd[g])
+
     barrier = pltpu.get_barrier_semaphore()
     for peer in (partner, cross, diag):
         pl.semaphore_signal(barrier, inc=1, device_id={"sp": peer}, device_id_type=MESH)
@@ -51,9 +66,13 @@
         slot = lax.rem(b + nb, NS)
         return load(v_hbm.at[b], ring.at[slot], ring_sem.at[slot])
 
+    small = [load(a, b, wt_sem.at[6 + i]) for i, (a, b) in enumerate(((hid_hbm, hid_ref), (ga_hbm, ga_ref), (len_hbm, len_ref), (u_hbm, u_ref), (w_hbm, w_ref), (gm_hbm, gm_ref)))]
+    for copy in small:
+        copy.start()
     wdt = wq_hbm.shape[1]
     stage = ring.at[NS - 2]
-    r_copy = load(r_hbm, ring.at[NS - 1], ring_sem.at[NS - 1])
+    step = 1024
+    r_copies = [load(r_hbm.at[:, pl.ds(c, step)], ring.at[NS - 1, :, pl.ds(c, step)], r_sem.at[c // step]) for c in range(0, width, step)]
     wq_copy = load(wq_hbm, stage.at[:, pl.ds(0, wdt)], wt_sem.at[0])
     wk_copy = load(wk_hbm, stage.at[:, pl.ds(wdt, wdt)], wt_sem.at[1])
     wv_copy = load(wv_hbm, stage.at[:, pl.ds(2 * wdt, wdt)], wt_sem.at[2])
@@ -61,14 +80,31 @@
     wu_copy = load(wu_hbm, wu, wt_sem.at[4])
     wd_copy = load(wd_hbm, wd, wt_sem.at[5])
     wq_copy.start()
-    r_copy.start()
+    for copy in r_copies:
+        copy.start()
     wk_copy.start()
     wv_copy.start()
     for b in range(NS - 2):
         k_load(b).start()
 
+    for copy in small:
+        copy.wait()
+    if compact:
+        for level in range(2):
+            rank = jnp.int32(0)
+            for b in range(nb):
+                table[level, b] = rank
+                rank = rank + (len_ref[b] >= (2 + level) * width).astype(jnp.int32)
+        reach = [len_ref[b] >= (2 + core) * width for b in range(nb)]
+        ranks = [table[core, b] for b in range(nb)]
+        chosen = {}
+        for g in range(STAGES):
+            for c in range(even[g + 1] - even[g]):
+                want = begin(g, core) + c
+                chosen[g, c] = functools.reduce(jnp.add, [jnp.where(reach[b] & (ranks[b] == want), b, 0) for b in range(nb)])
+
     hidden = hid_ref[...].astype(F32)
-    normed = rms(hidden, ga_ref[...].astype(F32))
+    normed = rms(hidden, ga_ref[...][None].astype(F32))
 
     head_of_row = lax.broadcasted_iota(jnp.int32, (nh, feat), 0)
     head_of_col = lax.broadcasted_iota(jnp.int32, (nh, feat), 1) // hd
@@ -90,10 +126,9 @@
         pos_rows.append(jnp.where(diag_mask, row + w_wide, 0.0))
     q_pos = jnp.concatenate(pos_rows, axis=0).astype(BF16)
 
-    r_copy.wait()
-    step = 1024
     for c in range(width // step):
         cols = pl.ds(c * step, step)
+        r_copies[c].wait()
         prod = jnp.dot(q_pos, ring[NS - 1, :, cols], preferred_element_type=F32)
         rel_own[:, :, cols] = prod.reshape(nb, nh, step)
     pl.semaphore_wait(barrier, 4)
@@ -101,17 +136,26 @@
     par_copy = pltpu.make_async_remote_copy(src_ref=rel_own, dst_ref=rel_par, send_sem=par_sem.at[0], recv_sem=par_sem.at[1],
                                             device_id={"sp": partner}, device_id_type=MESH)
 
-    def cross_copy(i):
-        return pltpu.make_async_remote_copy(src_ref=rel_own.at[i], dst_ref=rel_cro.at[i], send_sem=cro_send.at[i], recv_sem=cro_recv.at[i],
+    def cross_copy(g, c):
+        i = even[g] + c
+        return pltpu.make_async_remote_copy(src_ref=rel_send.at[i], dst_ref=rel_cro[g].at[c], send_sem=cro_send.at[i], recv_sem=cro_recv.at[i],
                                             device_id={"sp": cross}, device_id_type=MESH)
 
-    def forward_copy(i):
-        return pltpu.make_async_remote_copy(src_ref=rel_cro.at[i], dst_ref=rel_dia.at[i], send_sem=dia_send.at[i], recv_sem=dia_recv.at[i],
+    def forward_copy(g, c):
+        i = even[g] + c
+        return pltpu.make_async_remote_copy(src_ref=rel_cro[g].at[c], dst_ref=rel_dia[g].at[c], send_sem=dia_send.at[i], recv_sem=dia_recv.at[i],
                                             device_id={"sp": partner}, device_id_type=MESH)
 
-    par_copy.start()
-    for i in range(nb):
-        cross_copy(i).start()
+    for g in range(STAGES):
+        for c in range(even[g + 1] - even[g]):
+            if compact:
+                rel_send[even[g] + c] = rel_own[chosen[g, c]]
+
+            @pl.when(c < size(g, core))
+            def _():
+                cross_copy(g, c).start()
+        if g == 0:
+            par_copy.start()
 
     wk_copy.wait()
     k_new[...] = lax.dot_general(normed, stage[:, pl.ds(wdt, wdt)], NT, preferred_element_type=F32).astype(BF16).astype(F32)
@@ -120,8 +164,19 @@
     for b in range(NS - 2, NS):
         k_load(b).start()
 
+    def arrive(g, c):
+        @pl.when((c >= 0) & (c < size(g, core)))
+        def _():
+            cross_copy(g, c).wait()
+            forward_copy(g, c).start()
+
     @pl.loop(0, nb)
     def _(b):
+        @pl.when(b == nb - 3)
+        def _():
+            for c in range(rel_cro[0].shape[0]):
+                arrive(0, c)
+
         k_load(b).wait()
         content[b] = jnp.dot(qc_bd[b], ring[lax.rem(b, NS)], preferred_element_type=F32)[:nh]
 
@@ -133,9 +188,6 @@
         def _():
             v_load(b + NS - nb).start()
 
-    wo_copy.start()
-    wu_copy.start()
-    wd_copy.start()
     par_copy.wait()
 
     lane = lax.broadcasted_iota(jnp.int32, (nh, width), 1)
@@ -143,16 +195,28 @@
     stat_lane = lax.broadcasted_iota(jnp.int32, (nh, 128), 1)
     stat_row = lax.broadcasted_iota(jnp.int32, (nh, 128), 0)
 
-    def attend(b):
+    def pick(rows, g, b, level):
+        if not compact:
+            return rows[g][b - g * GROUP]
+        unit = table[level, b]
+        x = rows[0][jnp.minimum(unit, rows[0].shape[0] - 1)]
+        for h in range(1, g + 1):
+            local = unit - begin(h, level)
+            x = jnp.where(local >= 0, rows[h][jnp.clip(local, 0, rows[h].shape[0] - 1)], x)
+        return x
+
+    def score(g, b, slot):
         length = len_ref[b]
         high = length // width
         low = length - high * width
         first = high - sp
         upper = lane <= low
+        far = pick(rel_cro, g, b, core)
+        farther = pick(rel_dia, g, b, 1 - core)
         comb = jnp.zeros((nh, width), F32)
-        for block, rows in ((sp, rel_own), (partner, rel_par), (cross, rel_cro), (diag, rel_dia)):
+        for block, rows in ((sp, rel_own[b]), (partner, rel_par[b]), (cross, far), (diag, farther)):
             want = jnp.where(upper, first, first - 1) == block
-            comb = jnp.where(want, rows[b], comb)
+            comb = jnp.where(want, rows, comb)
         pieces = [jnp.take_along_axis(comb[:, 128 * c:128 * c + 128], back, axis=1) for c in range(width // 128)]
         relative = pltpu.roll(jnp.concatenate(pieces[::-1], axis=1), lax.rem(low + 1, width), axis=1)
         here = length - sp * width
@@ -166,30 +230,56 @@
         weights = jnp.where(valid, jnp.exp(scores - top), 0.0)
         total = jnp.sum(weights, axis=1, keepdims=True)
         p_new = jnp.sum(jnp.where(is_new, weights, 0.0), axis=1, keepdims=True).astype(BF16).astype(F32)
-        cached = jnp.where(is_new, 0.0, weights).astype(BF16)
-        slot = lax.rem(b + nb, NS)
-        v_load(b).wait()
-        mixed = lax.dot_general(cached, ring[slot], NT, preferred_element_type=F32)
-        mixed = mixed + p_new * v_new[pl.ds(b, 1), :]
-        rows_acc[b, :, pl.ds(0, feat)] = jnp.sum(jnp.where(diag_mask, mixed, 0.0), axis=0, keepdims=True)
+        probs[slot] = jnp.where(is_new, 0.0, weights).astype(BF16)
+        p_extra[slot] = jnp.broadcast_to(p_new, (nh, 128))
         stats = jnp.where(stat_lane == stat_row, top, jnp.where(stat_lane == stat_row + nh, total, 0.0))
         rows_acc[b, :, pl.ds(feat, 128)] = jnp.sum(stats, axis=0, keepdims=True)
 
-        @pl.when(b < nb - NS)
-        def _():
-            v_load(b + NS).start()
-
-    @pl.loop(0, nb + 1)
-    def _(i):
-        @pl.when(i < nb)
-        def _():
-            cross_copy(i).wait()
-            forward_copy(i).start()
-
-        @pl.when(i >= 1)
-        def _():
-            forward_copy(i - 1).wait()
-            attend(i - 1)
+    def mix(b, slot):
+        mixed = lax.dot_general(probs[slot], ring[lax.rem(b + nb, NS)], NT, preferred_element_type=F32)
+        mixed = mixed + p_extra[slot][:, :1] * v_new[pl.ds(b, 1), :]
+        rows_acc[b, :, pl.ds(0, feat)] = jnp.sum(jnp.where(diag_mask, mixed, 0.0), axis=0, keepdims=True)
+
+    def settle(g):
+        for c in range(rel_cro[g].shape[0]):
+            @pl.when(c < size(g, core))
+            def _():
+                forward_copy(g, c).wait_send()
+
+            @pl.when(c < size(g, 1 - core))
+            def _():
+                forward_copy(g, c).wait_recv()
+
+    settle(0)
+    score(0, 0, 0)
+
+    for g in range(nb // GROUP):
+        late = rel_cro[g + 1].shape[0] if g + 1 < STAGES else 0
+        first_step = max(g * GROUP - 1, 0)
+        last_step = g * GROUP + GROUP - 2
+        if g > 0:
+            settle(g)
+        for c in range(late - (last_step - first_step + 1)):
+            arrive(g + 1, c)
+
+        @pl.loop(first_step, last_step + 1)
+        def _(i):
+            if late:
+                arrive(g + 1, i - last_step + late - 1)
+
+            v_load(i).wait()
+            mix(i, lax.rem(i, 2))
+            score(g, i + 1, lax.rem(i + 1, 2))
+
+            @pl.when(i < nb - NS)
+            def _():
+                v_load(i + NS).start()
+
+    wo_copy.start()
+    wu_copy.start()
+    wd_copy.start()
+    v_load(nb - 1).wait()
+    mix(nb - 1, (nb - 1) % 2)
 
     for b in range(nb):
         part[0, b:b + 1, :] = rows_acc[b]
@@ -228,7 +318,7 @@
     swap.start()
     swap.wait()
     middle = (hidden + (attn + arecv[...])).astype(BF16).astype(F32)
-    normed_mlp = rms(middle, gm_ref[...].astype(F32))
+    normed_mlp = rms(middle, gm_ref[...][None].astype(F32))
     wu_copy.wait()
     up = jnp.dot(normed_mlp, wu[...], preferred_element_type=F32)
     act = jax.nn.gelu(up, approximate=True).astype(BF16)
@@ -255,35 +345,53 @@
         proj = [w.transpose(1, 2, 0).reshape(feat, model) for w in (w_query, w_key, w_value)]
         vmem = pl.BlockSpec(memory_space=pltpu.VMEM)
         hbm = pl.BlockSpec(memory_space=pl.ANY)
-        smem = pl.BlockSpec(memory_space=pltpu.SMEM)
         dma = pltpu.SemaphoreType.DMA
-        return pl.pallas_call(
-            kernel,
-            out_shape=jax.ShapeDtypeStruct((nb, model), BF16),
-            in_specs=[vmem, hbm, hbm, smem, hbm, vmem, vmem, vmem, hbm, hbm, hbm, hbm, vmem, hbm, hbm],
-            out_specs=vmem,
-            scratch_shapes=[
-                pltpu.VMEM((NS, feat, width), BF16),
-                pltpu.VMEM((nb, nh, width), F32),
-                pltpu.VMEM((nb, nh, width), F32),
-                pltpu.VMEM((nb, nh, width), F32),
-                pltpu.VMEM((nb, nh, width), F32),
-                pltpu.VMEM((nb, nh, width), F32),
-                pltpu.VMEM((feat, model), BF16),
-                pltpu.VMEM(w_up.shape, BF16),
-                pltpu.VMEM(w_down.shape, BF16),
-                pltpu.VMEM((nb, 16, feat), BF16),
-                pltpu.VMEM((nb, feat), F32),
-                pltpu.VMEM((nb, feat), F32),
-                pltpu.VMEM((nb, 1, feat + 128), F32),
-                pltpu.VMEM((4, nb, feat + 128), F32),
-                pltpu.VMEM((nb, model), F32),
-                pltpu.VMEM((nb, model), F32),
-                pltpu.VMEM((nb, model), F32),
-                pltpu.VMEM((nb, model), F32),
-                dma((NS,)), dma((6,)), dma((2,)), dma((nb,)), dma((nb,)), dma((nb,)), dma((nb,)), dma((4,)), dma((4,)), dma((4,)),
-            ],
-            compiler_params=pltpu.CompilerParams(collective_id=0, has_side_effects=True, vmem_limit_bytes=67043328),
-        )(hidden, k_t, v_t, lengths, r_t, u_bias, w_bias, g_attn[None], *proj, w_out.reshape(feat, model), g_mlp[None], w_up, w_down)
+        full = 2 * (tuple(range(0, nb + 1, nb // STAGES)),)
+        tight = (0, 4, 7, 10, 13), (0, 3, 5, 7, 8)
+
+        def call(caps, *operands):
+            compact = caps != full
+            rows = caps[0][-1]
+            return pl.pallas_call(
+                functools.partial(kernel, caps),
+                out_shape=jax.ShapeDtypeStruct((nb, model), BF16),
+                in_specs=15 * [hbm],
+                out_specs=vmem,
+                scratch_shapes=[
+                    pltpu.VMEM(hidden.shape, BF16),
+                    pltpu.SMEM(lengths.shape, jnp.int32),
+                    pltpu.VMEM(u_bias.shape, BF16),
+                    pltpu.VMEM(w_bias.shape, BF16),
+                    pltpu.VMEM(g_attn.shape, BF16),
+                    pltpu.VMEM(g_mlp.shape, BF16),
+                    pltpu.VMEM((NS, feat, width), BF16),
+                    pltpu.VMEM((nb, nh, width), F32),
+                    pltpu.VMEM((nb, nh, width), F32),
+                    pltpu.VMEM((nb, nh, width), F32),
+                    pltpu.VMEM((2, nh, width), BF16),
+                    pltpu.VMEM((2, nh, 128), F32),
+                    pltpu.VMEM((feat, model), BF16),
+                    pltpu.VMEM(w_up.shape, BF16),
+                    pltpu.VMEM(w_down.shape, BF16),
+                    pltpu.VMEM((nb, 16, feat), BF16),
+                    pltpu.VMEM((nb, feat), F32),
+                    pltpu.VMEM((nb, feat), F32),
+                    pltpu.VMEM((nb, 1, feat + 128), F32),
+                    pltpu.VMEM((4, nb, feat + 128), F32),
+                    pltpu.VMEM((nb, model), F32),
+                    pltpu.VMEM((nb, model), F32),
+                    pltpu.VMEM((nb, model), F32),
+                    pltpu.VMEM((nb, model), F32),
+                    dma((NS,)), dma((12,)), dma((4,)), dma((2,)), dma((rows,)), dma((rows,)), dma((rows,)), dma((rows,)), dma((4,)), dma((4,)), dma((4,)),
+                    pltpu.SMEM((2, nb), jnp.int32),
+                ] + 2 * [pltpu.VMEM((b - a, nh, width), F32) for a, b in zip(caps[0], caps[0][1:])] + ([pltpu.VMEM((rows, nh, width), F32)] if compact else []),
+                compiler_params=pltpu.CompilerParams(collective_id=int(compact), has_side_effects=True, vmem_limit_bytes=67043328),
+            )(*operands)
+
+        operands = (hidden, k_t, v_t, lengths, r_t, u_bias, w_bias, g_attn, *proj, w_out.reshape(feat, model), g_mlp, w_up, w_down)
+        seen = jnp.arange(nb)[:, None] < jnp.arange(nb // STAGES, nb + 1, nb // STAGES)[None]
+        counts = [jnp.sum(jnp.where((lengths >= level * width)[:, None] & seen, 1, 0), axis=0) for level in (2, 3)]
+        fits = functools.reduce(jnp.logical_and, [jnp.all(n <= jnp.array(cap[1:])) for n, cap in zip(counts, tight)])
+        return lax.cond(fits, functools.partial(call, tight), functools.partial(call, full), *operands)
 
     return jax.shard_map(layer_step, mesh=mesh, in_specs=in_specs, out_specs=P('dp', None), check_vma=False)

time: 72.7 us -> 65.4 us (0.90)
  Pallas kernels: 68.5 us -> 60.1 us
  local copies, waits for them, and re-layouts: 3.92 us -> 1.38 us
  other arithmetic: 0 us -> 2.24 us
  between operations: 0.01 us -> 1.36 us
    pallas_call x1, Pallas kernels: 68.5 us -> 60.1 us  [call(): pl.pallas_call(functools.partial(kernel, caps), out_shape=jax.ShapeDtypeS...]
    broadcast_in_dim x2 -> x0, local copies, waits for them, and re-layouts: 2.55 us -> none  [the longest x1 1.28 us: layer_step(): g_attn[None]]
    reduce_and x0 -> x1, other arithmetic: none -> 1.4 us  [layer_step(): jnp.all(n <= jnp.array(cap[1:]))]
where the time goes in v2:
time: 65.4 us; the launch traced here: 65.2 us
  Pallas kernels  60.1 us (92%)
  other arithmetic  2.24 us (3%)
  local copies, waits for them, and re-layouts  1.38 us (2%)
  between operations  1.36 us (2%)
    pallas_call x1, Pallas kernels, call(): pl.pallas_call(functools.partial(kernel, caps), out_shape=jax.ShapeDtypeS...  60.1 us
    reduce_and x1, other arithmetic, layer_step(): jnp.all(n <= jnp.array(cap[1:]))  1.4 us
    unnamed x1, local copies, waits for them, and re-layouts  1.38 us

profile of v2, /device:TPU:0, one launch (start us, length us, event | category | flops | bytes accessed | tf_op | source)
XLA Modules:
  0.0 65.2 jit_solution(5470414564599015232)
XLA Ops:
  0.0 0.7 %broadcast_compare_fusion.1 = (pred[16]{0:T(512)(128)(4,1)S(1)}, pred[16]{0:T(512)(128)(4,1)S(1)}) fusion(s32[16]{0:T(128)} %param.22), kind=kLoop, calls=%fused_computation.9 | loop fusion | flops 32 | bytes 96 | tf_op jit(solution)/shard_map/ge | solution.py:393
  0.7 0.2 select_reduce_fusion
  0.9 1.4 %compare_reduce_fusion = (pred[]{:T(512)}, pred[]{:T(512)}) fusion(s32[4]{0:T(128)S(1)} %get-tuple-element.145, s32[4]{0:T(128)} %constant.17.clone, s32[4]{0:T(128)S(1)} %get-tuple-element.146, s32[4]{0:T(128)} %constant.16.clone), kind=kLoop, calls=%fused_computation.5 | loop fusion | flops 14 | bytes 66 | tf_op jit(solution)/shard_map/reduce_and | solution.py:394
  3.6 60.3 %conditional.1 = (bf16[16,1024]{1,0:T(8,128)(2,1)}) conditional(s32[]{:T(128)} %convert_element_type.3, (bf16[16,1024]{1,0:T(8,128)(2,1)}, bf16[16,8,64,4096]{3,2,1,0:T(8,128)(2,1)}, bf16[16,8,64,4096]{3,2,1,0:T(8,128)(2,1)}, s32[16]{0:T(128)}, bf16[8,64,4096]{2,1,0:T(8,128)(2,1)}, /*index=5*/bf16[8,64]{1,0:T(8,128)(2,1)}, bf16[8,64]{1,0:T(8,128)(2,1)}, ...), branch_computations={%region_4.5_spmd, %region_5.6_spmd} | conditional | bytes 8 | solution.py:395
  3.8 60.1 %branch_1_fun.1 = bf16[16,1024]{1,0:T(8,128)(2,1)} custom-call(bf16[16,1024]{1,0:T(8,128)(2,1)} %get-tuple-element.128.hid_hbm, bf16[16,512,4096]{2,1,0:T(8,128)(2,1)} %bitcast.7.k_hbm, bf16[16,512,4096]{2,1,0:T(8,128)(2,1)} %bitcast.8.v_hbm, s32[16]{0:T(128)} %get-tuple-element.86.len_hbm, bf16[512,4096]{1,0:T(8,128)(2,1)} %bitcast.23, ...), custom_call_target="tpu_custom_call" | custom-call | tf_op jit(solution)/shard_map/cond/branch_1_fun/pallas_call | solution.py:355
  63.9 1.4 %copy.39 = bf16[16,1024]{1,0:T(8,128)(2,1)} copy(bf16[16,1024]{1,0:T(8,128)(2,1)} %get-tuple-element.98) | data formatting | bytes 65536
  (1 shorter events, 0.0 us)
